TPU v7x, 32 devices: a whole 2x2x4 slice. The times are simulated.
32 devices in a mesh: row: 4 (over y, x), col: 8 (over z, core).
Axes of the slice: x: 2, y: 2, z: 4, core: 2. Of those that a mesh axis runs over, the one named last changes fastest.
Arguments:
- view_one: bfloat16 [2048, 8192], P('row', 'col'), may hold values from -6 to 6
- view_two: bfloat16 [2048, 8192], P('row', 'col'), may hold values from -6 to 6
- pair_weights: bfloat16 [8192, 8192], P('row', 'col'), may hold values from 0.25 to 2.5
Outputs:
- first_grad: bfloat16 [2048, 8192], P('row', 'col')
- second_grad: bfloat16 [2048, 8192], P('row', 'col')
All inputs are finite; a program needn't handle non-finite values.
Results may differ from a plain program's by a relative error of at most 0.004.
Values may be sent and summed in bfloat16 or wider, within the bound.
A program may use at most 128 MiB of HBM per device.

v0:
```python
import jax
import jax.numpy as jnp
from jax import lax
from jax.sharding import PartitionSpec as P


def per_device(view_one, view_two, pair_weights):
    wide_two = lax.all_gather(view_two, "col", axis=1, tiled=True)
    samples = view_one.shape[0] * lax.axis_size("row")
    local_rows = pair_weights.shape[0]
    local_cols = pair_weights.shape[1]
    regrouped = lax.all_to_all(wide_two, "row", split_axis=1, concat_axis=0, tiled=True)
    summed = lax.dot_general(
        regrouped,
        lax.all_gather(view_one, "row", axis=0, tiled=True),
        (((0,), (0,)), ((), ())),
        preferred_element_type=jnp.float32,
    )
    correlation = summed / samples
    row_ids = lax.axis_index("row") * local_rows + lax.broadcasted_iota(
        jnp.int32, (local_rows, local_cols), 0
    )
    col_ids = lax.axis_index("col") * local_cols + lax.broadcasted_iota(
        jnp.int32, (local_rows, local_cols), 1
    )
    identity = jnp.where(row_ids == col_ids, 1.0, 0.0).astype(jnp.float32)
    weighted = (pair_weights.astype(jnp.float32) * (correlation - identity)).astype(jnp.bfloat16)
    grad_cols = lax.all_gather(weighted, "row", axis=0, tiled=True)
    first_grad = jnp.dot(wide_two, grad_cols, preferred_element_type=jnp.float32).astype(
        jnp.bfloat16
    )
    second_flipped = lax.psum_scatter(
        lax.dot_general(
            grad_cols, view_one, (((1,), (1,)), ((), ())), preferred_element_type=jnp.float32
        ),
        "col",
        scatter_dimension=0,
        tiled=True,
    )
    return (first_grad, second_flipped.T.astype(jnp.bfloat16))


def solution(mesh):
    placed = (P("row", "col"), P("row", "col"), P("row", "col"))
    return jax.shard_map(
        per_device,
        mesh=mesh,
        in_specs=placed,
        out_specs=(P("row", "col"), P("row", "col")),
        check_vma=False,
    )
```

profile of v0, /device:TPU:13, one launch (start us, length us, event | category | flops | bytes accessed | tf_op | source)
XLA Modules:
  0.0 602.0 jit_solution(17463055193101031785)
XLA Ops:
  8.0 0.0 all-gather.4.cloned.1.call-start
  8.0 2.3 copy.9
  10.3 0.0 all-gather.4.cloned.1.call-update
  10.3 81.8 %all-gather.4.cloned.1.call-done = bf16[512,8192]{0,1:T(8,128)(2,1)} async-done(((bf16[512,1024]{0,1:T(8,128)(2,1)}), bf16[512,8192]{0,1:T(8,128)(2,1)}) %all-gather.4.cloned.1.call-update) | async-done | bytes 8388624 | tf_op jit(solution)/shard_map/all_gather | solution.py:8
  92.1 5.7 all-to-all-start
  97.8 0.0 all-gather.6.cloned.1.call-start
  97.8 0.6 all-gather.6.cloned.1.call-update
  98.4 0.0 all-gather.8.cloned.1.call-start
  98.4 125.0 %all-to-all-done = bf16[512,4,2048]{0,2,1:T(8,128)(2,1)} async-done(((bf16[512,4,2048]{0,2,1:T(8,128)(2,1)}), bf16[512,4,2048]{0,2,1:T(8,128)(2,1)}, u32[]{:S(2)}, u32[]{:S(2)}) %all-to-all-start) | async-done | bytes 8388640 | tf_op jit(solution)/shard_map/all_to_all | solution.py:12
  223.4 11.4 %copy.10 = bf16[4,512,2048]{2,1,0:T(8,128)(2,1)} copy(bf16[4,512,2048]{1,2,0:T(8,128)(2,1)} %bitcast.1) | data formatting | bytes 16777216 | tf_op jit(solution)/shard_map/all_to_all | solution.py:12
  234.9 0.0 all-gather.6.cloned.1.call-done
  234.9 0.0 copy-start
  234.9 15.8 %multiply_convert_fusion = bf16[2048,1024]{1,0:T(8,128)(2,1)} fusion(bf16[2048,1024]{1,0:T(8,128)(2,1)} %param.5, bf16[2048,2048]{1,0:T(8,128)(2,1)} %bitcast.14, bf16[2048,1024]{1,0:T(8,128)(2,1)} %all-gather.6.cloned.1.call-done, s32[1024]{0:T(1024)S(1)} %iota_add_fusion.1, s32[2048]{0:T(1024)S(1)} %iota_add_fusion), kind=kOutput, calls=%fused_computation | convolution fusion | flops 8604614656 | bytes 20983808 | tf_op jit(solution)/shard_map/dot_general | solution.py:13
  250.7 0.0 all-gather.8.cloned.1.call-update
  250.7 0.2 reduce-scatter.2.cloned.1.call-start
  250.9 157.5 %all-gather.8.cloned.1.call-done = bf16[8192,1024]{1,0:T(8,128)(2,1)} async-done(((bf16[2048,1024]{1,0:T(8,128)(2,1)}), bf16[8192,1024]{1,0:T(8,128)(2,1)}) %all-gather.8.cloned.1.call-update) | async-done | bytes 16777232 | tf_op jit(solution)/shard_map/all_gather | solution.py:28
  408.4 0.0 copy-done
  408.4 15.8 %fusion.1 = f32[8192,512]{1,0:T(8,128)} fusion(bf16[8192,1024]{1,0:T(8,128)(2,1)} %all-gather.8.cloned.1.call-done, bf16[512,1024]{1,0:T(8,128)(2,1)S(1)} %copy-done), kind=kOutput, calls=%fused_computation.6 | convolution fusion | flops 8589934592 | bytes 34603008 | tf_op jit(solution)/shard_map/dot_general | solution.py:33
  424.2 0.0 reduce-scatter.2.cloned.1.call-update
  424.2 14.8 %fusion = bf16[512,1024]{0,1:T(8,128)(2,1)S(1)} fusion(bf16[8192,1024]{1,0:T(8,128)(2,1)} %all-gather.8.cloned.1.call-done, bf16[512,8192]{0,1:T(8,128)(2,1)} %all-gather.4.cloned.1.call-done), kind=kOutput, calls=%fused_computation.2 | convolution fusion | flops 8590458880 | bytes 26214400 | tf_op jit(solution)/shard_map/dot_general | solution.py:29
  439.0 1.3 copy.11
  440.4 151.2 %reduce-scatter.2.cloned.1.call-done = f32[1024,512]{1,0:T(8,128)} async-done(((f32[8192,512]{1,0:T(8,128)}), f32[1024,512]{1,0:T(8,128)}) %reduce-scatter.2.cloned.1.call-update) | async-done | bytes 2097168 | tf_op jit(solution)/shard_map/reduce_scatter | solution.py:32
  591.5 1.7 convert_bitcast_fusion
  593.3 1.3 copy.12
  (2 shorter events, 0.0 us)
Async XLA Ops:
  8.0 84.1 %all-gather.4.cloned.1.call-start = ((), (), s32[]{:S(2)}) async-start(), calls=%async_computation.2 | async-start | bytes 9437184 | tf_op jit(solution)/shard_map/all_gather | solution.py:8
  92.1 131.3 %all-to-all-start = ((bf16[512,4,2048]{0,2,1:T(8,128)(2,1)}), bf16[512,4,2048]{0,2,1:T(8,128)(2,1)}, u32[]{:S(2)}, u32[]{:S(2)}) async-start(bf16[512,4,2048]{0,2,1:T(8,128)(2,1)} %bitcast.13), calls=%async_computation | async-start | bytes 16777216 | tf_op jit(solution)/shard_map/all_to_all | solution.py:12
  97.8 137.1 %all-gather.6.cloned.1.call-start = ((), (), s32[]{:S(2)}) async-start(), calls=%async_computation.3 | async-start | bytes 5242880 | tf_op jit(solution)/shard_map/all_gather | solution.py:15
  98.4 310.1 %all-gather.8.cloned.1.call-start = ((), (), s32[]{:S(2)}) async-start(), calls=%async_computation.4 | async-start | bytes 20971520 | tf_op jit(solution)/shard_map/all_gather | solution.py:28
  234.9 173.6 %copy-start = (bf16[512,1024]{1,0:T(8,128)(2,1)S(1)}, bf16[512,1024]{1,0:T(8,128)(2,1)}, u32[]{:S(2)}) copy-start(bf16[512,1024]{1,0:T(8,128)(2,1)} %param.3) | copy-start | bytes 3145732
  250.7 340.8 %reduce-scatter.2.cloned.1.call-start = ((), (), s32[]{:S(2)}) async-start(), calls=%async_computation.5 | async-start | bytes 18874368 | tf_op jit(solution)/shard_map/reduce_scatter | solution.py:32
Sparse Core Ops, SparseCore 0:
  11.0 81.0 all-gather.3
  424.3 167.1 reduce-scatter.1
Sparse Core Ops, SparseCore 1:
  100.1 120.6 all-gather.5
  250.8 157.6 all-gather.7
where the time goes:
time: 605 us; the launch traced here: 602 us
  waiting for transfers between devices  516 us (85%)
  matrix products  46.4 us (8%)
  local copies, waits for them, and re-layouts  16.3 us (3%)
  between operations  15.5 us (3%)
    all_gather x1, waiting for transfers between devices, per_device(): grad_cols = lax.all_gather(weighted, 'row', axis=0, tiled=True)  158 us
    reduce_scatter x1, waiting for transfers between devices, per_device(): lax.psum_scatter(lax.dot_general(grad_cols, view_one, (((1,), (1,)), ((),...  151 us
    all_to_all x1, waiting for transfers between devices, per_device(): lax.all_to_all(wide_two, 'row', split_axis=1, concat_axis=0, tiled=True)  125 us
    all_gather x1, waiting for transfers between devices, per_device(): wide_two = lax.all_gather(view_two, 'col', axis=1, tiled=True)  81.8 us
    dot_general x1, matrix products, per_device(): lax.dot_general(regrouped, lax.all_gather(view_one, 'row', axis=0, tiled=...  15.8 us
    dot_general x1, matrix products, per_device(): lax.dot_general(grad_cols, view_one, (((1,), (1,)), ((), ())), preferred_...  15.8 us
    dot_general x1, matrix products, per_device(): jnp.dot(wide_two, grad_cols, preferred_element_type=jnp.float32)  14.8 us
  transfers between devices with their start and end apart: 5, of which 4 were waited for; matrix products, arithmetic and copies ran while one was open for 5% of the time, Pallas kernels for 0%

commit v1 on v0

v1 whole, which is shorter than its diff:
```python
import jax
import jax.numpy as jnp
from jax import lax
from jax.experimental import pallas as pl
from jax.experimental.pallas import tpu as pltpu
from jax.sharding import PartitionSpec as P

MESH = pl.DeviceIdType.MESH
CORES = 2


def arrived(ref, sem):
    pltpu.make_async_copy(ref, ref, sem).wait()


def gather_kernel(rows, one_ref, two_ref, one_out, two_out, one_held, held, load_sem, up_send, down_send,
                  held_recv, swap_send, swap_recv, one_send, one_recv, pair_send, pair_recv, twin_send, twin_recv):
    samples, width = two_ref.shape
    row, col = lax.axis_index("row"), lax.axis_index("col")
    z, core = lax.div(col, CORES), lax.rem(col, CORES)
    twin = (row, col + 1 - 2 * core)
    core_cols = pl.ds(pl.multiple_of(core * width, width), width)

    def block_rows(index):
        return pl.ds(pl.multiple_of(index * samples, samples), samples)

    def remote(src, dst, send, recv, device):
        return pltpu.make_async_remote_copy(
            src_ref=src, dst_ref=dst, send_sem=send, recv_sem=recv, device_id=device, device_id_type=MESH
        )

    def up(index):
        return remote(held.at[index], held.at[index], up_send.at[index], held_recv.at[index], (row, col + CORES))

    def down(index):
        return remote(held.at[index], held.at[index], down_send.at[index], held_recv.at[index], (row, col - CORES))

    def swap(index):
        return remote(held.at[index], two_out.at[block_rows(row), core_cols], swap_send.at[index],
                      swap_recv.at[row], (index, col))

    def route(index):
        @pl.when(index != row)
        def _():
            swap(index).start()

        @pl.when(index == row)
        def _():
            pltpu.make_async_copy(held.at[index], two_out.at[block_rows(row), core_cols], swap_recv.at[row]).start()

    def one_copy(step):
        target = lax.rem(row + step, rows)
        return remote(one_held, one_out.at[block_rows(row), pl.ds(0, width)], one_send.at[step], one_recv.at[row],
                      (target, col))

    def one_twin(index):
        part = one_out.at[block_rows(index), pl.ds(0, width)]
        return remote(part, one_out.at[block_rows(index), pl.ds(width, width)], pair_send.at[index],
                      pair_recv.at[index], twin)

    def two_twin(index):
        part = two_out.at[block_rows(index), core_cols]
        return remote(part, part, twin_send.at[index], twin_recv.at[index], twin)

    load_two = pltpu.make_async_copy(two_ref, held.at[z], load_sem.at[0])
    load_one = pltpu.make_async_copy(one_ref, one_held, load_sem.at[1])
    load_two.start()
    load_one.start()
    load_two.wait()

    @pl.when(z < rows - 1)
    def _():
        up(z).start()

    @pl.when(z > 0)
    def _():
        down(z).start()

    route(z)
    load_one.wait()
    for step in range(1, rows):
        one_copy(step).start()
    keep_one = pltpu.make_async_copy(one_held, one_out.at[block_rows(row), pl.ds(0, width)], one_recv.at[row])
    keep_one.start()

    for step in range(1, rows):
        @pl.when(z >= step)
        def _(step=step):
            index = z - step
            arrived(held.at[index], held_recv.at[index])

            @pl.when(z < rows - 1)
            def _():
                up(index).start()

            route(index)

        @pl.when(z + step < rows)
        def _(step=step):
            index = z + step
            arrived(held.at[index], held_recv.at[index])

            @pl.when(z > 0)
            def _():
                down(index).start()

            route(index)

    for step in range(rows):
        index = lax.rem(row - step + rows, rows)
        arrived(one_out.at[block_rows(index), pl.ds(0, width)], one_recv.at[index])
        one_twin(index).start()
    for step in range(rows):
        index = lax.rem(row - step + rows, rows)
        arrived(two_out.at[block_rows(index), core_cols], swap_recv.at[index])
        two_twin(index).start()

    twin_cols = pl.ds(pl.multiple_of((1 - core) * width, width), width)
    for index in range(rows):
        one_twin(index).wait_send()
        two_twin(index).wait_send()
        arrived(one_out.at[block_rows(index), pl.ds(width, width)], pair_recv.at[index])
        arrived(two_out.at[block_rows(index), twin_cols], twin_recv.at[index])

        @pl.when(index != row)
        def _(index=index):
            swap(index).wait_send()

        @pl.when(jnp.logical_and(z < rows - 1, index <= z))
        def _(index=index):
            up(index).wait_send()

        @pl.when(jnp.logical_and(z > 0, index >= z))
        def _(index=index):
            down(index).wait_send()
    for step in range(1, rows):
        one_copy(step).wait_send()


def scatter_kernel(rows, first_ref, second_ref, first_out, second_out, parts, moved, terms, first_send, first_recv,
                   move_send, move_recv, term_send, term_recv):
    samples, width = first_out.shape
    row, col = lax.axis_index("row"), lax.axis_index("col")
    z, core = lax.div(col, CORES), lax.rem(col, CORES)

    def block_rows(index):
        return pl.ds(pl.multiple_of(index * samples, samples), samples)

    def remote(src, dst, send, recv, device):
        return pltpu.make_async_remote_copy(
            src_ref=src, dst_ref=dst, send_sem=send, recv_sem=recv, device_id=device, device_id_type=MESH
        )

    def move(step):
        target = lax.rem(row + step, rows)
        return remote(second_ref.at[block_rows(target)], moved.at[row], move_send.at[step], move_recv.at[row],
                      (target, col))

    def first_copy(step):
        target = lax.rem(row + step, rows)
        return remote(first_ref.at[block_rows(target)], parts.at[row], first_send.at[step], first_recv.at[row],
                      (target, col))

    def term(step):
        target = lax.rem(z + step, rows)
        return remote(moved.at[target], terms.at[z], term_send.at[step], term_recv.at[z],
                      (row, target * CORES + core))

    for step in range(1, rows):
        move(step).start()
    pltpu.make_async_copy(second_ref.at[block_rows(row)], moved.at[row], move_recv.at[row]).start()
    for step in range(1, rows):
        first_copy(step).start()
    pltpu.make_async_copy(first_ref.at[block_rows(row)], parts.at[row], first_recv.at[row]).start()
    for step in range(1, rows):
        target = lax.rem(z + step, rows)
        arrived(moved.at[target], move_recv.at[target])
        term(step).start()
    arrived(moved.at[z], move_recv.at[z])
    for index in range(rows):
        arrived(parts.at[index], first_recv.at[index])

    chunk = 64

    def add_first(i, _):
        here = pl.ds(pl.multiple_of(i * chunk, chunk), chunk)
        total = parts[0, here, :].astype(jnp.float32)
        for index in range(1, rows):
            total += parts[index, here, :].astype(jnp.float32)
        first_out[here, :] = total.astype(first_out.dtype)
        return 0

    lax.fori_loop(0, samples // chunk, add_first, 0)
    for step in range(1, rows):
        source = lax.rem(z + step, rows)
        arrived(terms.at[source], term_recv.at[source])

    def add_second(i, _):
        here = pl.ds(pl.multiple_of(i * chunk, chunk), chunk)
        total = moved[z, here, :].astype(jnp.float32)
        for step in range(1, rows):
            total += terms[lax.rem(z + step, rows), here, :].astype(jnp.float32)
        second_out[here, :] = total.astype(second_out.dtype)
        return 0

    lax.fori_loop(0, samples // chunk, add_second, 0)
    for step in range(1, rows):
        move(step).wait_send()
        first_copy(step).wait_send()
        term(step).wait_send()


def gather(rows, view_one, view_two):
    samples, width = view_one.shape
    whole = jax.ShapeDtypeStruct((rows * samples, CORES * width), jnp.bfloat16)
    any_space = pl.BlockSpec(memory_space=pl.ANY)
    dma = pltpu.SemaphoreType.DMA
    return pl.pallas_call(
        lambda *refs: gather_kernel(rows, *refs),
        out_shape=(whole, whole),
        in_specs=[any_space] * 2,
        out_specs=(any_space, any_space),
        scratch_shapes=[
            pltpu.VMEM((samples, width), jnp.bfloat16),
            pltpu.VMEM((rows, samples, width), jnp.bfloat16),
            dma((2,)),
        ] + [dma((rows,))] * 11,
        compiler_params=pltpu.CompilerParams(has_side_effects=True),
        name="gather_views",
    )(view_one, view_two)


def scatter(rows, first, second):
    samples, width = first.shape[0] // rows, first.shape[1]
    own = jax.ShapeDtypeStruct((samples, width), jnp.bfloat16)
    any_space = pl.BlockSpec(memory_space=pl.ANY)
    vmem = pl.BlockSpec(memory_space=pltpu.VMEM)
    blocks = pltpu.VMEM((rows, samples, width), jnp.bfloat16)
    return pl.pallas_call(
        lambda *refs: scatter_kernel(rows, *refs),
        out_shape=(own, own),
        in_specs=[any_space] * 2,
        out_specs=(vmem, vmem),
        scratch_shapes=[blocks, blocks, blocks] + [pltpu.SemaphoreType.DMA((rows,))] * 6,
        compiler_params=pltpu.CompilerParams(has_side_effects=True, vmem_limit_bytes=40 * 2**20),
        name="scatter_grads",
    )(first, second)


def per_device(view_one, view_two, pair_weights):
    rows = lax.axis_size("row")
    samples = view_one.shape[0] * rows
    local_rows, local_cols = pair_weights.shape
    row, col = lax.axis_index("row"), lax.axis_index("col")
    core = lax.rem(col, CORES)
    one_pair, two_rows = gather(rows, view_one, view_two)
    summed = lax.dot_general(
        two_rows, one_pair[:, :local_cols], (((0,), (0,)), ((), ())), preferred_element_type=jnp.float32
    )
    row_ids = row * local_rows + lax.broadcasted_iota(jnp.int32, (local_rows, local_cols), 0)
    col_ids = col * local_cols + lax.broadcasted_iota(jnp.int32, (local_rows, local_cols), 1)
    identity = jnp.where(row_ids == col_ids, 1.0, 0.0).astype(jnp.float32)
    weighted = (pair_weights.astype(jnp.float32) * (summed / samples - identity)).astype(jnp.bfloat16)
    mine = lax.dynamic_slice_in_dim(weighted, core * local_cols, local_cols, 0)
    other = lax.dynamic_slice_in_dim(weighted, (1 - core) * local_cols, local_cols, 0)
    pairs = [(i, i + 1 - 2 * (i % CORES)) for i in range(lax.axis_size("col"))]
    theirs = lax.ppermute(other, "col", pairs)
    first = jnp.dot(two_rows, weighted, preferred_element_type=jnp.float32).astype(jnp.bfloat16)
    across = jnp.concatenate([mine, theirs], axis=1)
    second = lax.dot_general(
        one_pair, across, (((1,), (1,)), ((), ())), preferred_element_type=jnp.float32
    ).astype(jnp.bfloat16)
    return scatter(rows, first, second)


def solution(mesh):
    placed = (P("row", "col"), P("row", "col"), P("row", "col"))
    return jax.shard_map(
        per_device,
        mesh=mesh,
        in_specs=placed,
        out_specs=(P("row", "col"), P("row", "col")),
        check_vma=False,
    )
```

time: 605 us -> 319 us (0.53)
  waiting for transfers between devices: 516 us -> 0.01 us
  Pallas kernels: 0 us -> 274 us
  between operations: 15.5 us -> 0.75 us
  matrix products: 46.4 us -> 35.1 us
  local copies, waits for them, and re-layouts: 16.3 us -> 8.99 us
    pallas_call x0 -> x2, Pallas kernels: none -> 274 us  [the longest x1 167 us: scatter(): pl.pallas_call(lambda *refs: scatter_kernel(rows, *refs), out_shape=(own,...]
    all_gather x3 -> x0, waiting for transfers between devices: 239 us -> none  [the longest x1 158 us: per_device(): grad_cols = lax.all_gather(weighted, 'row', axis=0, tiled=True)]
    reduce_scatter x1 -> x0, waiting for transfers between devices: 151 us -> none  [per_device(): lax.psum_scatter(lax.dot_general(grad_cols, view_one, (((1,), (1,)), ((),...]
    all_to_all x1 -> x0, waiting for transfers between devices: 125 us -> none  [per_device(): lax.all_to_all(wide_two, 'row', split_axis=1, concat_axis=0, tiled=True)]
    all_to_all x1 -> x0, local copies, waits for them, and re-layouts: 11.4 us -> none  [per_device(): lax.all_to_all(wide_two, 'row', split_axis=1, concat_axis=0, tiled=True)]
    dot_general x3, matrix products: 46.4 us -> 35.1 us  [the longest x1 14.4 us: per_device(): lax.dot_general(two_rows, one_pair[:, :local_cols], (((0,), (0,)), ((), (...]
  transfers between devices with their start and end apart: 5 -> 1, of which waited for: 4 -> 0; matrix products, arithmetic and copies ran while one was open for 5% -> 4% of each run, Pallas kernels for 0% -> 0%
where the time goes in v1:
time: 319 us
  Pallas kernels  274 us (86%)
  matrix products  35.1 us (11%)
  local copies, waits for them, and re-layouts  8.99 us (3%)
    pallas_call x1, Pallas kernels, scatter(): pl.pallas_call(lambda *refs: scatter_kernel(rows, *refs), out_shape=(own,...  167 us
    pallas_call x1, Pallas kernels, gather(): pl.pallas_call(lambda *refs: gather_kernel(rows, *refs), out_shape=(whole...  106 us
    dot_general x1, matrix products, per_device(): lax.dot_general(two_rows, one_pair[:, :local_cols], (((0,), (0,)), ((), (...  14.4 us
    dot_general x1, matrix products, per_device(): jnp.dot(two_rows, weighted, preferred_element_type=jnp.float32)  11.4 us
    dot_general x1, matrix products, per_device(): lax.dot_general(one_pair, across, (((1,), (1,)), ((), ())), preferred_ele...  9.3 us
    unnamed x7, local copies, waits for them, and re-layouts  8.44 us
  transfers between devices with their start and end apart: 1, of which 0 were waited for; matrix products, arithmetic and copies ran while one was open for 4% of the time, Pallas kernels for 0%

profile of v1, /device:TPU:13, one launch (start us, length us, event | category | flops | bytes accessed | tf_op | source)
XLA Modules:
  0.0 318.7 jit_solution(3818574023012756519)
XLA Ops:
  0.6 6.5 %copy.5 = bf16[2048,1024]{0,1:T(8,128)(2,1)} copy(bf16[2048,1024]{1,0:T(8,128)(2,1)} %param.5) | data formatting | bytes 8388608 | tf_op args[2]
  7.1 106.5 %gather_views.1 = (bf16[2048,2048]{1,0:T(8,128)(2,1)}, bf16[2048,2048]{1,0:T(8,128)(2,1)}) custom-call(bf16[512,1024]{1,0:T(8,128)(2,1)} %refs_0_.1, bf16[512,1024]{1,0:T(8,128)(2,1)} %refs_1_.1), custom_call_target="tpu_custom_call" | custom-call | tf_op jit(solution)/shard_map/gather_views/pallas_call | solution.py:218
  113.6 14.4 %multiply_convert_fusion = bf16[2048,1024]{0,1:T(8,128)(2,1)S(1)} fusion(bf16[2048,1024]{0,1:T(8,128)(2,1)} %copy.5, bf16[2048,2048]{1,0:T(8,128)(2,1)} %get-tuple-element.4, s32[2048]{0:T(1024)S(1)} %iota_add_fusion, bf16[2048,2048]{1,0:T(8,128)(2,1)} %get-tuple-element.5, s32[1024]{0:T(1024)S(1)} %iota_add_fusion.1), kind=kOutput, calls=%fused_computation | convolution fusion | flops 8604614656 | bytes 20983808 | tf_op jit(solution)/shard_map/dot_general | solution.py:257
  128.0 0.5 constant_dynamic-slice_fusion.1
  128.6 0.0 slice-start
  128.6 0.0 slice-start.1
  128.6 0.2 collective-permute-start
  128.8 11.4 %convolution_convert_fusion.refs_0_ = bf16[2048,1024]{1,0:T(8,128)(2,1)S(1)} fusion(bf16[2048,2048]{1,0:T(8,128)(2,1)} %get-tuple-element.4, bf16[2048,1024]{0,1:T(8,128)(2,1)S(1)} %multiply_convert_fusion), kind=kOutput, calls=%fused_computation.7 | convolution fusion | flops 8592031744 | bytes 16777216 | tf_op jit(solution)/shard_map/dot_general | solution.py:268
  140.2 0.0 collective-permute-done
  140.2 0.0 slice-done
  140.3 0.0 slice-done.1
  140.3 9.3 %fusion.5.refs_1_ = bf16[2048,1024]{1,0:T(8,128)(2,1)S(1)} fusion(bf16[2048,2048]{1,0:T(8,128)(2,1)S(1)} %bitcast.5, bf16[1024,1024]{0,1:T(8,128)(2,1)S(1)} %collective-permute-done, bf16[1024,1024]{0,1:T(8,128)(2,1)S(1)} %get-tuple-element.6), kind=kOutput, calls=%fused_computation.6 | convolution fusion | flops 8600420352 | bytes 16777216 | tf_op jit(solution)/shard_map/dot_general | solution.py:270
  149.6 167.1 %scatter_grads.1 = (bf16[512,1024]{1,0:T(8,128)(2,1)S(1)}, bf16[512,1024]{1,0:T(8,128)(2,1)S(1)}) custom-call(bf16[2048,1024]{1,0:T(8,128)(2,1)S(1)} %convolution_convert_fusion.refs_0_, bf16[2048,1024]{1,0:T(8,128)(2,1)S(1)} %fusion.5.refs_1_), custom_call_target="tpu_custom_call" | custom-call | tf_op jit(solution)/shard_map/scatter_grads/pallas_call | solution.py:239
  316.7 1.0 copy.8
  317.7 1.0 copy.9
  (3 shorter events, 0.0 us)
Async XLA Ops:
  128.6 11.7 %slice-start = ((s8[8388608]{0:T(1024)(128)(4,1)}), s8[4194304]{0:T(1024)(128)(4,1)S(1)}, s32[]{:S(2)}) async-start(s8[8388608]{0:T(1024)(128)(4,1)} %bitcast.4), calls=%async_computation | async-start | bytes 8388608
  128.6 11.7 %slice-start.1 = ((s8[8388608]{0:T(1024)(128)(4,1)}), s8[4194304]{0:T(1024)(128)(4,1)S(1)}, s32[]{:S(2)}) async-start(s8[8388608]{0:T(1024)(128)(4,1)} %bitcast.4), calls=%async_computation.1 | async-start | bytes 8388608
  128.6 11.6 %collective-permute-start = (bf16[1024,1024]{0,1:T(8,128)(2,1)S(1)}, bf16[1024,1024]{0,1:T(8,128)(2,1)S(1)}, u32[]{:S(2)}, u32[]{:S(2)}) collective-permute-start(bf16[1024,1024]{0,1:T(8,128)(2,1)S(1)} %get-tuple-element.7), channel_id=1, source_target_pairs={{0,1},{1,0},{2,3},{3,2},{4,5},{5,4},{6,7},{7,6},{8,9},{9,8},{10,11... | collective-permute-start | bytes 6291464 | tf_op jit(solution)/shard_map/ppermute | solution.py:267

commit v2 on v0

v2 whole, which is shorter than its diff:
```python
import jax
import jax.numpy as jnp
from jax import lax
from jax.experimental import pallas as pl
from jax.experimental.pallas import tpu as pltpu
from jax.sharding import PartitionSpec as P

MESH = pl.DeviceIdType.MESH
CORES = 2
PIECES = 4


def arrived(ref, sem):
    pltpu.make_async_copy(ref, ref, sem).wait()


def remote(src, dst, send, recv, device):
    return pltpu.make_async_remote_copy(
        src_ref=src, dst_ref=dst, send_sem=send, recv_sem=recv, device_id=device, device_id_type=MESH
    )


def gather_kernel(rows, one_ref, two_ref, one_out, two_out, one_held, held, load_sem, one_send, one_recv, pair_send,
                  pair_recv, up_send, down_send, held_recv, swap_send, swap_recv, twin_send, twin_recv):
    samples, width = two_ref.shape
    piece = samples // PIECES
    row, col = lax.axis_index("row"), lax.axis_index("col")
    z, core = lax.div(col, CORES), lax.rem(col, CORES)
    twin = (row, col + 1 - 2 * core)
    core_cols = pl.ds(pl.multiple_of(core * width, width), width)
    twin_cols = pl.ds(pl.multiple_of((1 - core) * width, width), width)

    def block_rows(index):
        return pl.ds(pl.multiple_of(index * samples, samples), samples)

    def piece_rows(index, q):
        return pl.ds(pl.multiple_of(index * samples + q * piece, piece), piece)

    def held_piece(index, q):
        return held.at[index, pl.ds(q * piece, piece)]

    def up(index, q):
        part = held_piece(index, q)
        return remote(part, part, up_send.at[index, q], held_recv.at[index, q], (row, col + CORES))

    def down(index, q):
        part = held_piece(index, q)
        return remote(part, part, down_send.at[index, q], held_recv.at[index, q], (row, col - CORES))

    def swap(index, q):
        return remote(held_piece(index, q), two_out.at[piece_rows(row, q), core_cols], swap_send.at[index, q],
                      swap_recv.at[row, q], (index, col))

    def route(index, q):
        @pl.when(index != row)
        def _():
            swap(index, q).start()

        @pl.when(index == row)
        def _():
            pltpu.make_async_copy(held_piece(index, q), two_out.at[piece_rows(row, q), core_cols],
                                  swap_recv.at[row, q]).start()

    def one_copy(step):
        target = lax.rem(row + step, rows)
        return remote(one_held, one_out.at[block_rows(row), pl.ds(0, width)], one_send.at[step], one_recv.at[row],
                      (target, col))

    def one_twin(index):
        part = one_out.at[block_rows(index), pl.ds(0, width)]
        return remote(part, one_out.at[block_rows(index), pl.ds(width, width)], pair_send.at[index],
                      pair_recv.at[index], twin)

    def two_twin(index, q):
        part = two_out.at[piece_rows(index, q), core_cols]
        return remote(part, part, twin_send.at[index, q], twin_recv.at[index, q], twin)

    def pass_up(index, q):
        @pl.when(z < rows - 1)
        def _():
            up(index, q).start()

    def pass_down(index, q):
        @pl.when(z > 0)
        def _():
            down(index, q).start()

    def own(q):
        pass_up(z, q)
        pass_down(z, q)
        route(z, q)

    load_two = pltpu.make_async_copy(two_ref, held.at[z], load_sem.at[0])
    load_one = pltpu.make_async_copy(one_ref, one_held, load_sem.at[1])
    load_two.start()
    load_one.start()
    load_two.wait()
    own(0)
    load_one.wait()
    for step in range(1, rows):
        one_copy(step).start()
    pltpu.make_async_copy(one_held, one_out.at[block_rows(row), pl.ds(0, width)], one_recv.at[row]).start()

    for q in range(PIECES):
        if q + 1 < PIECES:
            own(q + 1)
        for step in range(1, rows):
            @pl.when(z >= step)
            def _(step=step, q=q):
                arrived(held_piece(z - step, q), held_recv.at[z - step, q])
                pass_up(z - step, q)
                route(z - step, q)

            @pl.when(z + step < rows)
            def _(step=step, q=q):
                arrived(held_piece(z + step, q), held_recv.at[z + step, q])
                pass_down(z + step, q)
                route(z + step, q)

    for step in range(rows):
        index = lax.rem(row - step + rows, rows)
        arrived(one_out.at[block_rows(index), pl.ds(0, width)], one_recv.at[index])
        one_twin(index).start()
    for q in range(PIECES):
        for step in range(rows):
            index = lax.rem(row - step + rows, rows)
            arrived(two_out.at[piece_rows(index, q), core_cols], swap_recv.at[index, q])
            two_twin(index, q).start()

    for index in range(rows):
        one_twin(index).wait_send()
        arrived(one_out.at[block_rows(index), pl.ds(width, width)], pair_recv.at[index])
        for q in range(PIECES):
            two_twin(index, q).wait_send()
            arrived(two_out.at[piece_rows(index, q), twin_cols], twin_recv.at[index, q])

            @pl.when(index != row)
            def _(index=index, q=q):
                swap(index, q).wait_send()

            @pl.when(jnp.logical_and(z < rows - 1, index <= z))
            def _(index=index, q=q):
                up(index, q).wait_send()

            @pl.when(jnp.logical_and(z > 0, index >= z))
            def _(index=index, q=q):
                down(index, q).wait_send()
    for step in range(1, rows):
        one_copy(step).wait_send()


def scatter_kernel(rows, one_ref, two_ref, weighted_ref, first_out, second_out, one_held, two_held, weighted, theirs,
                   first_sent, parts, second_sent, moved, from_below, from_above, load_sem, twin_sem, first_send,
                   first_recv, move_send, move_recv, up_send, up_recv, down_send, down_recv):
    samples, width = first_out.shape
    tile = width // PIECES
    row, col = lax.axis_index("row"), lax.axis_index("col")
    z, core = lax.div(col, CORES), lax.rem(col, CORES)

    def half(which):
        return pl.ds(pl.multiple_of(which * width, width), width)

    def move(target, q):
        return remote(second_sent.at[q, target], moved.at[q, row], move_send.at[q, target], move_recv.at[q, row],
                      (target, col))

    def first_copy(target, q):
        return remote(first_sent.at[q, target], parts.at[q, row], first_send.at[q, target], first_recv.at[q, row],
                      (target, col))

    def up(index, q):
        return remote(moved.at[q, index], from_below.at[q, index], up_send.at[q, index], up_recv.at[q, index],
                      (row, col + CORES))

    def down(index, q):
        return remote(moved.at[q, index], from_above.at[q, index], down_send.at[q, index], down_recv.at[q, index],
                      (row, col - CORES))

    def first_tile(target, q):
        cols = pl.ds(pl.multiple_of(q * tile, tile), tile)
        mine = two_held[pl.ds(pl.multiple_of(target * samples, samples), samples), :]
        return jnp.dot(mine, weighted[:, cols], preferred_element_type=jnp.float32).astype(jnp.bfloat16)

    def second_tile(target, q):
        here = pl.ds(pl.multiple_of(target * samples, samples), samples)
        contract = (((1,), (1,)), ((), ()))
        near = weighted[pl.ds(pl.multiple_of(core * width + q * tile, tile), tile), :]
        far = theirs[pl.ds(pl.multiple_of(q * tile, tile), tile), :]
        total = lax.dot_general(one_held[here, pl.ds(0, width)], near, contract, preferred_element_type=jnp.float32)
        total += lax.dot_general(one_held[here, pl.ds(width, width)], far, contract,
                                 preferred_element_type=jnp.float32)
        return total.astype(jnp.bfloat16)

    exchange = remote(weighted_ref.at[half(1 - core)], theirs, twin_sem.at[0], twin_sem.at[1],
                      (row, col + 1 - 2 * core))
    exchange.start()
    loads = [pltpu.make_async_copy(src, dst, load_sem.at[i]) for i, (src, dst) in enumerate(
        ((weighted_ref, weighted), (two_ref, two_held), (one_ref, one_held)))]
    for load in loads:
        load.start()
    loads[0].wait()
    loads[1].wait()

    def own_first(q, _):
        parts[q, row] = first_tile(row, q)
        return 0

    lax.fori_loop(0, PIECES, own_first, 0)
    loads[2].wait()
    exchange.wait()

    def seconds(i, _):
        q, step = lax.div(i, rows), lax.rem(i, rows) + 1
        target = lax.rem(row + step, rows)
        value = second_tile(target, q)

        @pl.when(target == row)
        def _():
            moved[q, row] = value

        @pl.when(target != row)
        def _():
            second_sent[q, target] = value
            move(target, q).start()

        return 0

    lax.fori_loop(0, PIECES * rows, seconds, 0)

    def firsts(i, _):
        q, step = lax.div(i, rows - 1), lax.rem(i, rows - 1) + 1
        target = lax.rem(row + step, rows)
        first_sent[q, target] = first_tile(target, q)
        first_copy(target, q).start()
        return 0

    lax.fori_loop(0, PIECES * (rows - 1), firsts, 0)

    def settle(index, q):
        @pl.when(index != row)
        def _():
            arrived(moved.at[q, index], move_recv.at[q, index])

    def chain(i, _):
        q, turn = lax.div(i, rows - 1), lax.rem(i, rows - 1)
        above = rows - 1 - (turn - z)
        below = turn - (rows - 1 - z)

        @pl.when(jnp.logical_and(turn >= z, above > z))
        def _():
            settle(above, q)

            @pl.when(z > 0)
            def _():
                arrived(from_below.at[q, above], up_recv.at[q, above])
                moved[q, above] = (moved[q, above].astype(jnp.float32)
                                   + from_below[q, above].astype(jnp.float32)).astype(jnp.bfloat16)

            up(above, q).start()

        @pl.when(jnp.logical_and(below >= 0, below < z))
        def _():
            settle(below, q)

            @pl.when(z < rows - 1)
            def _():
                arrived(from_above.at[q, below], down_recv.at[q, below])
                moved[q, below] = (moved[q, below].astype(jnp.float32)
                                   + from_above[q, below].astype(jnp.float32)).astype(jnp.bfloat16)

            down(below, q).start()

        return 0

    lax.fori_loop(0, PIECES * (rows - 1), chain, 0)

    for q in range(PIECES):
        cols = pl.ds(q * tile, tile)
        for step in range(1, rows):
            index = lax.rem(row + step, rows)
            arrived(parts.at[q, index], first_recv.at[q, index])
        total = parts[q, 0].astype(jnp.float32)
        for index in range(1, rows):
            total += parts[q, index].astype(jnp.float32)
        first_out[:, cols] = total.astype(first_out.dtype)
    for q in range(PIECES):
        cols = pl.ds(q * tile, tile)
        settle(z, q)

        @pl.when(z > 0)
        def _(q=q):
            arrived(from_below.at[q, z], up_recv.at[q, z])

        @pl.when(z < rows - 1)
        def _(q=q):
            arrived(from_above.at[q, z], down_recv.at[q, z])

        @pl.when(z == 0)
        def _(q=q, cols=cols):
            second_out[:, cols] = (moved[q, z].astype(jnp.float32)
                                   + from_above[q, z].astype(jnp.float32)).astype(second_out.dtype)

        @pl.when(z == rows - 1)
        def _(q=q, cols=cols):
            second_out[:, cols] = (moved[q, z].astype(jnp.float32)
                                   + from_below[q, z].astype(jnp.float32)).astype(second_out.dtype)

        @pl.when(jnp.logical_and(z > 0, z < rows - 1))
        def _(q=q, cols=cols):
            second_out[:, cols] = (moved[q, z].astype(jnp.float32) + from_below[q, z].astype(jnp.float32)
                                   + from_above[q, z].astype(jnp.float32)).astype(second_out.dtype)

    for q in range(PIECES):
        for step in range(1, rows):
            target = lax.rem(row + step, rows)
            move(target, q).wait_send()
            first_copy(target, q).wait_send()
        for index in range(rows):
            @pl.when(index > z)
            def _(index=index, q=q):
                up(index, q).wait_send()

            @pl.when(index < z)
            def _(index=index, q=q):
                down(index, q).wait_send()


def gather(rows, view_one, view_two):
    samples, width = view_one.shape
    whole = jax.ShapeDtypeStruct((rows * samples, CORES * width), jnp.bfloat16)
    any_space = pl.BlockSpec(memory_space=pl.ANY)
    dma = pltpu.SemaphoreType.DMA
    return pl.pallas_call(
        lambda *refs: gather_kernel(rows, *refs),
        out_shape=(whole, whole),
        in_specs=[any_space] * 2,
        out_specs=(any_space, any_space),
        scratch_shapes=[
            pltpu.VMEM((samples, width), jnp.bfloat16),
            pltpu.VMEM((rows, samples, width), jnp.bfloat16),
            dma((2,)),
        ] + [dma((rows,))] * 4 + [dma((rows, PIECES))] * 7,
        compiler_params=pltpu.CompilerParams(has_side_effects=True),
        name="gather_views",
    )(view_one, view_two)


def scatter(rows, one_pair, two_rows, weighted):
    height, width = weighted.shape
    samples = one_pair.shape[0] // rows
    own = jax.ShapeDtypeStruct((samples, width), jnp.bfloat16)
    any_space = pl.BlockSpec(memory_space=pl.ANY)
    vmem = pl.BlockSpec(memory_space=pltpu.VMEM)
    blocks = pltpu.VMEM((PIECES, rows, samples, width // PIECES), jnp.bfloat16)
    views = pltpu.VMEM(one_pair.shape, jnp.bfloat16)
    dma = pltpu.SemaphoreType.DMA
    return pl.pallas_call(
        lambda *refs: scatter_kernel(rows, *refs),
        out_shape=(own, own),
        in_specs=[any_space] * 3,
        out_specs=(vmem, vmem),
        scratch_shapes=[
            views,
            views,
            pltpu.VMEM((height, width), jnp.bfloat16),
            pltpu.VMEM((width, width), jnp.bfloat16),
        ] + [blocks] * 6 + [dma((3,)), dma((2,))] + [dma((PIECES, rows))] * 8,
        compiler_params=pltpu.CompilerParams(has_side_effects=True, vmem_limit_bytes=60 * 2**20),
        name="scatter_grads",
    )(one_pair, two_rows, weighted)


def per_device(view_one, view_two, pair_weights):
    rows = lax.axis_size("row")
    samples = view_one.shape[0] * rows
    local_rows, local_cols = pair_weights.shape
    row, col = lax.axis_index("row"), lax.axis_index("col")
    one_pair, two_rows = gather(rows, view_one, view_two)
    summed = lax.dot_general(
        two_rows, one_pair[:, :local_cols], (((0,), (0,)), ((), ())), preferred_element_type=jnp.float32
    )
    row_ids = row * local_rows + lax.broadcasted_iota(jnp.int32, (local_rows, local_cols), 0)
    col_ids = col * local_cols + lax.broadcasted_iota(jnp.int32, (local_rows, local_cols), 1)
    identity = jnp.where(row_ids == col_ids, 1.0, 0.0).astype(jnp.float32)
    weighted = (pair_weights.astype(jnp.float32) * (summed / samples - identity)).astype(jnp.bfloat16)
    return scatter(rows, one_pair, two_rows, weighted)


def solution(mesh):
    placed = (P("row", "col"), P("row", "col"), P("row", "col"))
    return jax.shard_map(
        per_device,
        mesh=mesh,
        in_specs=placed,
        out_specs=(P("row", "col"), P("row", "col")),
        check_vma=False,
    )
```

time: 605 us -> 236 us (0.39)
  waiting for transfers between devices: 516 us -> 0 us
  Pallas kernels: 0 us -> 212 us
  matrix products: 46.4 us -> 16.4 us
  between operations: 15.5 us -> 0.67 us
  local copies, waits for them, and re-layouts: 16.3 us -> 4.52 us
    all_gather x3 -> x0, waiting for transfers between devices: 239 us -> none  [the longest x1 158 us: per_device(): grad_cols = lax.all_gather(weighted, 'row', axis=0, tiled=True)]
    pallas_call x0 -> x2, Pallas kernels: none -> 212 us  [the longest x1 108 us: scatter(): pl.pallas_call(lambda *refs: scatter_kernel(rows, *refs), out_shape=(own,...]
    reduce_scatter x1 -> x0, waiting for transfers between devices: 151 us -> none  [per_device(): lax.psum_scatter(lax.dot_general(grad_cols, view_one, (((1,), (1,)), ((),...]
    all_to_all x1 -> x0, waiting for transfers between devices: 125 us -> none  [per_device(): lax.all_to_all(wide_two, 'row', split_axis=1, concat_axis=0, tiled=True)]
    dot_general x3 -> x1, matrix products: 46.4 us -> 16.4 us  [per_device(): lax.dot_general(two_rows, one_pair[:, :local_cols], (((0,), (0,)), ((), (...]
    all_to_all x1 -> x0, local copies, waits for them, and re-layouts: 11.4 us -> none  [per_device(): lax.all_to_all(wide_two, 'row', split_axis=1, concat_axis=0, tiled=True)]
  transfers between devices with their start and end apart: 5 -> 0, of which waited for: 4 -> 0; matrix products, arithmetic and copies ran while one was open for 5% -> 0% of each run, Pallas kernels for 0% -> 0%
where the time goes in v2:
time: 236 us; the launch traced here: 234 us
  Pallas kernels  212 us (90%)
  matrix products  16.4 us (7%)
  local copies, waits for them, and re-layouts  4.52 us (2%)
    pallas_call x1, Pallas kernels, scatter(): pl.pallas_call(lambda *refs: scatter_kernel(rows, *refs), out_shape=(own,...  108 us
    pallas_call x1, Pallas kernels, gather(): pl.pallas_call(lambda *refs: gather_kernel(rows, *refs), out_shape=(whole...  104 us
    dot_general x1, matrix products, per_device(): lax.dot_general(two_rows, one_pair[:, :local_cols], (((0,), (0,)), ((), (...  16.4 us

profile of v2, /device:TPU:13, one launch (start us, length us, event | category | flops | bytes accessed | tf_op | source)
XLA Modules:
  0.0 233.8 jit_solution(10162655978969572213)
XLA Ops:
  0.7 104.0 %gather_views.1 = (bf16[2048,2048]{1,0:T(8,128)(2,1)}, bf16[2048,2048]{1,0:T(8,128)(2,1)}) custom-call(bf16[512,1024]{1,0:T(8,128)(2,1)} %refs_0_.1, bf16[512,1024]{1,0:T(8,128)(2,1)} %refs_1_.1), custom_call_target="tpu_custom_call" | custom-call | tf_op jit(solution)/shard_map/gather_views/pallas_call | solution.py:333
  104.7 16.4 %multiply_convert_fusion.refs_2_ = bf16[2048,1024]{1,0:T(8,128)(2,1)} fusion(bf16[2048,1024]{1,0:T(8,128)(2,1)} %param.5, bf16[2048,2048]{1,0:T(8,128)(2,1)} %get-tuple-element.5.refs_1_, s32[1024]{0:T(1024)S(1)} %iota_add_fusion.1, bf16[2048,2048]{1,0:T(8,128)(2,1)} %get-tuple-element.4.refs_0_, s32[2048]{0:T(1024)S(1)} %iota_add_fusion), kind=kOutput, calls=%fused_computation | convolution fusion | flops 8604614656 | bytes 20983808 | tf_op jit(solution)/shard_map/dot_general | solution.py:379
  121.0 108.3 %scatter_grads.1 = (bf16[512,1024]{1,0:T(8,128)(2,1)}, bf16[512,1024]{1,0:T(8,128)(2,1)}) custom-call(bf16[2048,2048]{1,0:T(8,128)(2,1)} %get-tuple-element.4.refs_0_, bf16[2048,2048]{1,0:T(8,128)(2,1)} %get-tuple-element.5.refs_1_, bf16[2048,1024]{1,0:T(8,128)(2,1)} %multiply_convert_fusion.refs_2_), custom_call_target="tpu_custom_call" | custom-call | tf_op jit(solution)/shard_map/scatter_grads/pallas_call | solution.py:357
  229.3 2.3 copy.7
  231.5 2.3 copy.8
  (2 shorter events, 0.0 us)
